TPU v7x, 512 devices: a whole 4x8x8 slice. The times are simulated.
512 devices in a mesh: mem: 32 (over z_hi, y, core), kvh: 4 (over z_lo), row: 4 (over x).
Axes of the slice: x: 4, y: 8, z: 8 (z_hi: 2, z_lo: 4; z = z_hi * 4 + z_lo), core: 2. Of those that a mesh axis runs over, the one named last changes fastest.
Arguments:
- queries: bfloat16 [1024, 8192], P(('mem', 'kvh', 'row')), may hold values from -120 to 120
- output_gradient: bfloat16 [1024, 8192], P(('mem', 'kvh', 'row')), may hold values from -6 to 6
- keys: bfloat16 [24576, 1024], P('mem', 'kvh'), may hold values from -6 to 6
- values: bfloat16 [24576, 1024], P('mem', 'kvh'), may hold values from -6 to 6
- text_video: int32 [128, 8], P(None, 'row'), may hold values from 0 to 95
- video_blocks: int32 [96], replicated, may hold values from 1 to 4, 192 in all
Outputs:
- attention_out: bfloat16 [1024, 8192], P(('mem', 'kvh', 'row'))
- query_grad: bfloat16 [1024, 8192], P(('mem', 'kvh', 'row'))
- keys_gradient: bfloat16 [24576, 1024], P('mem', 'kvh')
- values_gradient: bfloat16 [24576, 1024], P('mem', 'kvh')
Inputs may be any that keep to these rules, and one draw needn't show every extreme that they name: Row sees images 0 to text_video. `video_blocks`: they sum to 192.
All inputs are finite; a program needn't handle non-finite values.
Results may differ from a plain program's by a relative error of at most 0.015.
Values may be sent and summed in bfloat16 or wider, within the bound.
A program may use at most 64 MiB of HBM per device.

v0:
```python
import jax
import jax.numpy as jnp
from jax import lax
from jax.sharding import PartitionSpec as P

QUERY_HEADS = 64
KEY_VALUE_HEADS = 8
HEAD_WIDTH = 128
FRAME = 128
masked_score = -1e30


def in_one_piece(arrays, axis, dim, along):
    both = jnp.concatenate(arrays, axis=along)
    result, at, outs = (lax.all_gather(both, axis, axis=dim, tiled=True), 0, [])
    for a in arrays:
        outs.append(lax.slice_in_dim(result, at, at + a.shape[along], axis=along))
        at += a.shape[along]
    return tuple(outs)


def sent_to_all(array, axis):
    count = lax.axis_size(axis)
    return lax.all_to_all(
        jnp.broadcast_to(array[None], (count, *array.shape)), axis, 0, 0, tiled=True
    )


def of_everyone(array, axis):
    everything = sent_to_all(array, axis)
    return jnp.sum(everything.astype(jnp.float32), axis=0)


def cut_along(array, dim, count):
    before, after = (array.shape[:dim], array.shape[dim + 1 :])
    return jnp.moveaxis(array.reshape(*before, count, -1, *after), dim, 0)


def sent_and_summed(array, axis, dim):
    pieces = cut_along(array, dim, lax.axis_size(axis))
    arrived = lax.all_to_all(pieces, axis, split_axis=0, concat_axis=0, tiled=True)
    return arrived.astype(jnp.float32).sum(axis=0)


def video_of_block(video_blocks, first_block, block_count):
    block_ends = jnp.cumsum(video_blocks)
    blocks = first_block + jnp.arange(block_count, dtype=jnp.int32)
    return jnp.sum((block_ends[None, :] <= blocks[:, None]).astype(jnp.int32), axis=1)


def per_device(queries, output_gradient, keys, values, text_video, video_blocks):
    inverse_root = HEAD_WIDTH ** (-0.5)
    heads_per_group = QUERY_HEADS // KEY_VALUE_HEADS
    mem_count = lax.axis_size("mem")
    local_query, local_grad = (
        lax.all_to_all(queries, "kvh", split_axis=1, concat_axis=0, tiled=True),
        lax.all_to_all(output_gradient, "kvh", split_axis=1, concat_axis=0, tiled=True),
    )
    query_rows, grad_rows = in_one_piece((local_query, local_grad), "mem", 0, 1)
    group_size = query_rows.shape[0]
    own_count = local_query.shape[0]
    key_local = keys.shape[1] // HEAD_WIDTH
    frames = keys.shape[0] // FRAME
    query_four = query_rows.reshape(group_size, key_local, heads_per_group, HEAD_WIDTH)
    grad_four = grad_rows.reshape(group_size, key_local, heads_per_group, HEAD_WIDTH)
    key_frames = keys.reshape(frames, FRAME, key_local, HEAD_WIDTH)
    value_frames = values.reshape(frames, FRAME, key_local, HEAD_WIDTH)
    key_video = video_of_block(video_blocks, lax.axis_index("mem") * frames, frames)
    visible = key_video[None, :] <= text_video.reshape(group_size)[:, None]
    frame_ids = jnp.arange(frames, dtype=jnp.int32)

    def frame_scores(frame_index):
        key_block = lax.dynamic_index_in_dim(key_frames, frame_index, 0, keepdims=False)
        scores = (
            jnp.einsum("rghd,jgd->rghj", query_four, key_block, preferred_element_type=jnp.float32)
            * inverse_root
        )
        seen_rows = lax.dynamic_index_in_dim(visible, frame_index, 1, keepdims=False)[
            :, None, None, None
        ]
        return (jnp.where(seen_rows, scores, masked_score), seen_rows, key_block)

    def forward_step(running, frame_index):
        running_top, totals, numerator = running
        scores, seen_rows, key_block = frame_scores(frame_index)
        new_top = jnp.maximum(running_top, jnp.max(scores, axis=3))
        weight = jnp.where(seen_rows, jnp.exp(scores - new_top[..., None]), 0.0)
        shrink_factor = jnp.exp(running_top - new_top)
        totals = totals * shrink_factor + jnp.sum(weight, axis=3)
        value_block = lax.dynamic_index_in_dim(value_frames, frame_index, 0, keepdims=False)
        numerator = numerator * shrink_factor[..., None] + jnp.einsum(
            "rghj,jgd->rghd",
            weight.astype(jnp.bfloat16),
            value_block,
            preferred_element_type=jnp.float32,
        )
        return ((new_top, totals, numerator), None)

    stat_shape = (group_size, key_local, heads_per_group)
    start_state = (
        jnp.full(stat_shape, masked_score, jnp.float32),
        jnp.zeros(stat_shape, jnp.float32),
        jnp.zeros(stat_shape + (HEAD_WIDTH,), jnp.float32),
    )
    (local_top, local_totals, numerator), unused = lax.scan(forward_step, start_state, frame_ids)
    own_grad = local_grad.reshape(own_count, key_local, heads_per_group, HEAD_WIDTH).astype(
        jnp.float32
    )
    sent = (
        numerator.reshape((mem_count, own_count) + numerator.shape[1:]),
        local_top.reshape((mem_count, own_count) + stat_shape[1:]),
        local_totals.reshape((mem_count, own_count) + stat_shape[1:]),
    )
    numerator_src, top_src, totals_src = (
        lax.all_to_all(sent[0], "mem", split_axis=0, concat_axis=0, tiled=True),
        lax.all_to_all(sent[1], "mem", split_axis=0, concat_axis=0, tiled=True),
        lax.all_to_all(sent[2], "mem", split_axis=0, concat_axis=0, tiled=True),
    )
    own_top = jnp.max(top_src, axis=0)
    factor = jnp.exp(top_src - own_top)
    own_totals = jnp.sum(totals_src * factor, axis=0)
    attention = jnp.sum(numerator_src * factor[..., None], axis=0) / own_totals[..., None]
    delta_own = jnp.sum(own_grad * attention, axis=3)
    own_log = own_top + jnp.log(own_totals)
    log_mass, delta_rows = in_one_piece((own_log, delta_own), "mem", 0, 1)
    attention_low = attention.reshape(own_count, key_local * heads_per_group * HEAD_WIDTH).astype(
        jnp.bfloat16
    )

    def backward_step(query_grad, frame_index):
        scores, seen_rows, key_block = frame_scores(frame_index)
        value_block = lax.dynamic_index_in_dim(value_frames, frame_index, 0, keepdims=False)
        probability = jnp.where(seen_rows, jnp.exp(scores - log_mass[..., None]), 0.0)
        prob_grad = jnp.einsum(
            "rghd,jgd->rghj", grad_four, value_block, preferred_element_type=jnp.float32
        )
        score_grad = (probability * (prob_grad - delta_rows[..., None])).astype(jnp.bfloat16)
        query_grad = (
            query_grad
            + jnp.einsum(
                "rghj,jgd->rghd", score_grad, key_block, preferred_element_type=jnp.float32
            )
            * inverse_root
        )
        key_part = (
            jnp.einsum("rghj,rghd->jgd", score_grad, query_four, preferred_element_type=jnp.float32)
            * inverse_root
        )
        value_part = jnp.einsum(
            "rghj,rghd->jgd",
            probability.astype(jnp.bfloat16),
            grad_four,
            preferred_element_type=jnp.float32,
        )
        return (query_grad, (key_part, value_part))

    query_grad, (key_parts, value_parts) = lax.scan(
        backward_step, jnp.zeros(stat_shape + (HEAD_WIDTH,), jnp.float32), frame_ids
    )
    key_sum = key_parts.reshape(keys.shape)
    value_sum = value_parts.reshape(values.shape)
    key_sum, value_sum = (
        of_everyone(key_sum.astype(jnp.bfloat16), "row").astype(jnp.float32),
        of_everyone(value_sum.astype(jnp.bfloat16), "row").astype(jnp.float32),
    )
    own_query_grad = sent_and_summed(query_grad.astype(jnp.bfloat16), "mem", 0)
    query_low = own_query_grad.reshape(own_count, key_local * heads_per_group * HEAD_WIDTH).astype(
        jnp.bfloat16
    )
    attention_text, query_text = (
        lax.all_to_all(attention_low, "kvh", split_axis=0, concat_axis=1, tiled=True),
        lax.all_to_all(query_low, "kvh", split_axis=0, concat_axis=1, tiled=True),
    )
    return (
        attention_text,
        query_text,
        key_sum.astype(jnp.bfloat16),
        value_sum.astype(jnp.bfloat16),
    )


def solution(mesh):
    in_specs = (
        P(("mem", "kvh", "row"), None),
        P(("mem", "kvh", "row"), None),
        P("mem", "kvh"),
        P("mem", "kvh"),
        P(None, "row"),
        P(),
    )
    out_specs = (
        P(("mem", "kvh", "row"), None),
        P(("mem", "kvh", "row"), None),
        P("mem", "kvh"),
        P("mem", "kvh"),
    )
    return jax.shard_map(
        per_device, mesh=mesh, in_specs=in_specs, out_specs=out_specs, check_vma=False
    )
```

profile of v0, /device:TPU:8, one launch (start us, length us, event | category | flops | bytes accessed | tf_op | source)
XLA Modules:
  0.0 536.6 jit_solution(9227071309435036342)
XLA Ops:
  7.2 13.1 %all_to_all.100 = bf16[2,4,2048]{2,0,1:T(2,128)(2,1)S(1)} all-to-all(bf16[2,4,2048]{2,0,1:T(2,128)(2,1)} %bitcast.198), channel_id=1, replica_groups=mesh['mem'=32,'kvh'=4,'row'=4] {'kvh'}, dimensions={1} | all-to-all | bytes 65536 | tf_op jit(solution)/shard_map/all_to_all | solution.py:57
  23.6 5.5 %all-to-all-done = bf16[2,4,2048]{2,0,1:T(2,128)(2,1)S(1)} async-done(((bf16[2,4,2048]{2,0,1:T(2,128)(2,1)}), bf16[2,4,2048]{2,0,1:T(2,128)(2,1)S(1)}, u32[]{:S(2)}, u32[]{:S(2)}) %all-to-all-start) | async-done | bytes 32800 | tf_op jit(solution)/shard_map/all_to_all | solution.py:56
  32.0 93.0 %all-gather.2.cloned.1.call-done = bf16[256,4096]{1,0:T(8,128)(2,1)} async-done(((bf16[8,4096]{1,0:T(8,128)(2,1)}), bf16[256,4096]{1,0:T(8,128)(2,1)}) %all-gather.2.cloned.1.call-update) | async-done | bytes 2097168 | tf_op jit(solution)/shard_map/all_gather | solution.py:15
  129.6 50.9 %while.30 = (s32[]{:T(128)}, f32[256,2,8]{0,2,1:T(8,128)S(1)}, f32[256,2,8]{0,2,1:T(8,128)S(1)}, f32[256,2,8,128]{0,3,2,1:T(8,128)}, s32[6]{0:T(128)S(1)}, /*ind...) while((s32[]{:T(128)}, f32[256,2,8]{0,2,1:T(8,128)S(1)}, ...), condition=%wide.region_5.6_spmd.clone, body=%wide.region_2.5_spmd.clone.sunk | while | flops 276844544 | bytes 12191419 | solution.py:105
  141.8 3.7 bitcast_add_fusion.4
  150.6 3.7 bitcast_add_fusion.4
  159.3 3.7 bitcast_add_fusion.4
  168.1 3.7 bitcast_add_fusion.4
  176.8 3.7 bitcast_add_fusion.4
  183.3 5.6 %all-to-all-start.3 = ((f32[32,1,128]{2,1,0:T(1,128)}), f32[32,1,128]{2,1,0:T(1,128)S(1)}, u32[]{:S(2)}, u32[]{:S(2)}) async-start(f32[32,1,128]{2,1,0:T(1,128)} %reshape.134), calls=%async_computation.3 | async-start | bytes 32768 | tf_op jit(solution)/shard_map/all_to_all | solution.py:116
  191.7 8.3 %all-to-all-done.3 = f32[32,1,128]{2,1,0:T(1,128)S(1)} async-done(((f32[32,1,128]{2,1,0:T(1,128)}), f32[32,1,128]{2,1,0:T(1,128)S(1)}, u32[]{:S(2)}, u32[]{:S(2)}) %all-to-all-start.3) | async-done | bytes 16416 | tf_op jit(solution)/shard_map/all_to_all | solution.py:116
  200.0 4.9 all-to-all-start.4
  206.9 9.2 %all-to-all-done.4 = f32[32,1,128]{2,1,0:T(1,128)S(1)} async-done(((f32[32,1,128]{2,1,0:T(1,128)}), f32[32,1,128]{2,1,0:T(1,128)S(1)}, u32[]{:S(2)}, u32[]{:S(2)}) %all-to-all-start.4) | async-done | bytes 16416 | tf_op jit(solution)/shard_map/all_to_all | solution.py:117
  216.7 5.1 all-to-all-start.2
  228.7 50.4 %all-to-all-done.2 = f32[32,8,2,8,128]{4,3,2,1,0:T(8,128)S(1)} async-done(((f32[32,8,2,8,128]{4,3,2,1,0:T(8,128)}), f32[32,8,2,8,128]{4,3,2,1,0:T(8,128)S(1)}, u32[]{:S(2)}, u32[]{:S(2)}) %all-to-all-start.2) | async-done | bytes 2097184 | tf_op jit(solution)/shard_map/all_to_all | solution.py:115
  280.1 46.2 %all_gather.7 = f32[256,4,8]{2,1,0:T(4,128)S(1)} all-gather(f32[8,4,8]{2,1,0:T(4,128)S(1)} %copy.109), channel_id=1, replica_groups=mesh['mem'=32,'kvh'=4,'row'=4] {'mem'}, dimensions={0}, use_global_device_ids=true | all-gather | bytes 33792 | tf_op jit(solution)/shard_map/all_gather | solution.py:15
  327.3 3.9 all-to-all-start.5
  331.2 87.4 %while.31 = (s32[]{:T(128)}, f32[256,2,8,128]{0,3,2,1:T(8,128)}, bf16[6,128,2,128]{3,1,2,0:T(8,128)(2,1)}, bf16[6,128,2,128]{3,1,2,0:T(8,128)(2,1)}, s32[6]{0:T(...) while((s32[]{:T(128)}, f32[256,2,8,128]{0,3,2,1:T(8,128)}, ...), condition=%wide.region_11.12_spmd.clone, body=%wide.region_10.11_spmd.clone.sunk | while | flops 676888576 | bytes 22776864 | solution.py:157
  421.4 4.5 all-to-all-start.8
  427.8 19.5 %all-to-all-done.8 = bf16[4,768,256]{2,1,0:T(8,128)(2,1)} async-done(((bf16[4,768,256]{2,1,0:T(8,128)(2,1)}), bf16[4,768,256]{2,1,0:T(8,128)(2,1)}, u32[]{:S(2)}, u32[]{:S(2)}) %all-to-all-start.8) | async-done | bytes 1572896 | tf_op jit(solution)/shard_map/all_to_all | solution.py:24
  447.3 12.5 %all-to-all-start.6 = ((bf16[32,8,2,8,128]{4,3,2,1,0:T(8,128)(2,1)}), bf16[32,8,2,8,128]{4,3,2,1,0:T(8,128)(2,1)S(1)}, u32[]{:S(2)}, u32[]{:S(2)}) async-start(bf16[32,8,2,8,128]{4,3,2,1,0:T(8,128)(2,1)} %bitcast.10), calls=%async_computation.6 | async-start | bytes 2097152 | tf_op jit(solution)/shard_map/all_to_all | solution.py:41
  461.2 31.6 %all-to-all-done.6 = bf16[32,8,2,8,128]{4,3,2,1,0:T(8,128)(2,1)S(1)} async-done(((bf16[32,8,2,8,128]{4,3,2,1,0:T(8,128)(2,1)}), bf16[32,8,2,8,128]{4,3,2,1,0:T(8,128)(2,1)S(1)}, u32[]{:S(2)}, u32[]{:S(2)}) %all-to-all-start.6) | async-done | bytes 1048608 | tf_op jit(solution)/shard_map/all_to_all | solution.py:41
  498.5 18.8 %all-to-all-done.9 = bf16[4,768,256]{2,1,0:T(8,128)(2,1)S(1)} async-done(((bf16[4,768,256]{2,1,0:T(8,128)(2,1)}), bf16[4,768,256]{2,1,0:T(8,128)(2,1)S(1)}, u32[]{:S(2)}, u32[]{:S(2)}) %all-to-all-start.9) | async-done | bytes 1572896 | tf_op jit(solution)/shard_map/all_to_all | solution.py:24
  517.2 4.8 all-to-all-start.7
  (255 shorter events, 141.8 us)
Async XLA Ops:
  7.2 23.9 %copy-start.4 = (bf16[768,256]{1,0:T(8,128)(2,1)S(1)}, bf16[768,256]{1,0:T(8,128)(2,1)}, u32[]{:S(2)}) copy-start(bf16[768,256]{1,0:T(8,128)(2,1)} %param.13) | copy-start | bytes 1179652
  7.2 24.0 %copy-start.11 = (s32[96]{0:T(128)S(1)}, s32[96]{0:T(128)}, u32[]{:S(2)}) copy-start(s32[96]{0:T(128)} %param.15) | copy-start | bytes 1156
  7.2 24.3 %copy-start.10 = (s32[128,2]{0,1:T(2,128)S(1)}, s32[128,2]{0,1:T(2,128)}, u32[]{:S(2)}) copy-start(s32[128,2]{0,1:T(2,128)} %param.14) | copy-start | bytes 3076
  20.3 8.9 %all-to-all-start = ((bf16[2,4,2048]{2,0,1:T(2,128)(2,1)}), bf16[2,4,2048]{2,0,1:T(2,128)(2,1)S(1)}, u32[]{:S(2)}, u32[]{:S(2)}) async-start(bf16[2,4,2048]{2,0,1:T(2,128)(2,1)} %bitcast.199), calls=%async_computation | async-start | bytes 65536 | tf_op jit(solution)/shard_map/all_to_all | solution.py:56
  23.5 101.5 %all-gather.2.cloned.1.call-start = ((), (), s32[]{:S(2)}) async-start(), calls=%async_computation.10 | async-start | bytes 2162688 | tf_op jit(solution)/shard_map/all_gather | solution.py:15
  180.6 26.4 %copy-start.3 = (bf16[6,128,2,128]{3,2,1,0:T(2,128)(2,1)}, bf16[6,128,2,128]{3,2,1,0:T(2,128)(2,1)S(1)}, u32[]{:S(2)}) copy-start(bf16[6,128,2,128]{3,2,1,0:T(2,128)(2,1)S(1)} %get-tuple-element.573) | copy-start | bytes 1179652
  180.6 26.4 %copy-start.6 = (pred[256,6]{0,1:T(8,128)(4,1)}, pred[256,6]{0,1:T(8,128)(4,1)S(1)}, u32[]{:S(2)}) copy-start(pred[256,6]{0,1:T(8,128)(4,1)S(1)} %get-tuple-element.579) | copy-start | bytes 4612
  180.6 24.4 %copy-start.2 = (f32[256,2,8,128]{0,3,2,1:T(8,128)S(1)}, f32[256,2,8,128]{0,3,2,1:T(8,128)}, u32[]{:S(2)}) copy-start(f32[256,2,8,128]{0,3,2,1:T(8,128)} %get-tuple-element.117) | copy-start | bytes 6291460
  183.3 16.7 %all-to-all-start.3 = ((f32[32,1,128]{2,1,0:T(1,128)}), f32[32,1,128]{2,1,0:T(1,128)S(1)}, u32[]{:S(2)}, u32[]{:S(2)}) async-start(f32[32,1,128]{2,1,0:T(1,128)} %reshape.134), calls=%async_computation.3 | async-start | bytes 32768 | tf_op jit(solution)/shard_map/all_to_all | solution.py:116
  200.0 16.1 %all-to-all-start.4 = ((f32[32,1,128]{2,1,0:T(1,128)}), f32[32,1,128]{2,1,0:T(1,128)S(1)}, u32[]{:S(2)}, u32[]{:S(2)}) async-start(f32[32,1,128]{2,1,0:T(1,128)} %reshape.136), calls=%async_computation.4 | async-start | bytes 32768 | tf_op jit(solution)/shard_map/all_to_all | solution.py:117
  216.7 62.3 %all-to-all-start.2 = ((f32[32,8,2,8,128]{4,3,2,1,0:T(8,128)}), f32[32,8,2,8,128]{4,3,2,1,0:T(8,128)S(1)}, u32[]{:S(2)}, u32[]{:S(2)}) async-start(f32[32,8,2,8,128]{4,3,2,1,0:T(8,128)} %bitcast.186), calls=%async_computation.2 | async-start | bytes 4194304 | tf_op jit(solution)/shard_map/all_to_all | solution.py:115
  228.3 51.5 %copy-start.5 = (f32[8,2,8,128]{3,2,1,0:T(8,128)S(1)}, f32[8,2,8,128]{3,2,1,0:T(8,128)}, u32[]{:S(2)}) copy-start(f32[8,2,8,128]{3,2,1,0:T(8,128)} %reshape.123) | copy-start | bytes 196612
  327.3 92.7 %all-to-all-start.5 = ((bf16[4,2,2048]{2,1,0:T(2,128)(2,1)}), bf16[4,2,2048]{2,1,0:T(2,128)(2,1)}, u32[]{:S(2)}, u32[]{:S(2)}) async-start(bf16[4,2,2048]{2,1,0:T(2,128)(2,1)} %convert_element_type.60), calls=%async_computation.5 | async-start | bytes 65536 | tf_op jit(solution)/shard_map/all_to_all | solution.py:171
  331.2 6.2 %copy-start.8 = (f32[256,2,8]{0,2,1:T(8,128)}, f32[256,2,8]{0,2,1:T(8,128)S(1)}, u32[]{:S(2)}) copy-start(f32[256,2,8]{0,2,1:T(8,128)S(1)} %get-tuple-element.549) | copy-start | bytes 49156 | tf_op jit(solution)/shard_map/while
  344.5 6.2 %copy-start.8 = (f32[256,2,8]{0,2,1:T(8,128)}, f32[256,2,8]{0,2,1:T(8,128)S(1)}, u32[]{:S(2)}) copy-start(f32[256,2,8]{0,2,1:T(8,128)S(1)} %get-tuple-element.549) | copy-start | bytes 49156 | tf_op jit(solution)/shard_map/while
  359.3 6.2 %copy-start.8 = (f32[256,2,8]{0,2,1:T(8,128)}, f32[256,2,8]{0,2,1:T(8,128)S(1)}, u32[]{:S(2)}) copy-start(f32[256,2,8]{0,2,1:T(8,128)S(1)} %get-tuple-element.549) | copy-start | bytes 49156 | tf_op jit(solution)/shard_map/while
  374.1 6.2 %copy-start.8 = (f32[256,2,8]{0,2,1:T(8,128)}, f32[256,2,8]{0,2,1:T(8,128)S(1)}, u32[]{:S(2)}) copy-start(f32[256,2,8]{0,2,1:T(8,128)S(1)} %get-tuple-element.549) | copy-start | bytes 49156 | tf_op jit(solution)/shard_map/while
  388.9 6.2 %copy-start.8 = (f32[256,2,8]{0,2,1:T(8,128)}, f32[256,2,8]{0,2,1:T(8,128)S(1)}, u32[]{:S(2)}) copy-start(f32[256,2,8]{0,2,1:T(8,128)S(1)} %get-tuple-element.549) | copy-start | bytes 49156 | tf_op jit(solution)/shard_map/while
  403.8 6.2 %copy-start.8 = (f32[256,2,8]{0,2,1:T(8,128)}, f32[256,2,8]{0,2,1:T(8,128)S(1)}, u32[]{:S(2)}) copy-start(f32[256,2,8]{0,2,1:T(8,128)S(1)} %get-tuple-element.549) | copy-start | bytes 49156 | tf_op jit(solution)/shard_map/while
  420.1 5.8 %copy-start.1 = (f32[256,2,8,128]{0,3,2,1:T(8,128)S(1)}, f32[256,2,8,128]{0,3,2,1:T(8,128)}, u32[]{:S(2)}) copy-start(f32[256,2,8,128]{0,3,2,1:T(8,128)} %get-tuple-element.120) | copy-start | bytes 6291460
  421.4 25.9 %all-to-all-start.8 = ((bf16[4,768,256]{2,1,0:T(8,128)(2,1)}), bf16[4,768,256]{2,1,0:T(8,128)(2,1)}, u32[]{:S(2)}, u32[]{:S(2)}) async-start(bf16[4,768,256]{2,1,0:T(8,128)(2,1)} %broadcast_in_dim.79), calls=%async_computation.8 | async-start | bytes 3145728 | tf_op jit(solution)/shard_map/all_to_all | solution.py:24
  447.3 45.6 %all-to-all-start.6 = ((bf16[32,8,2,8,128]{4,3,2,1,0:T(8,128)(2,1)}), bf16[32,8,2,8,128]{4,3,2,1,0:T(8,128)(2,1)S(1)}, u32[]{:S(2)}, u32[]{:S(2)}) async-start(bf16[32,8,2,8,128]{4,3,2,1,0:T(8,128)(2,1)} %bitcast.10), calls=%async_computation.6 | async-start | bytes 2097152 | tf_op jit(solution)/shard_map/all_to_all | solution.py:41
  494.1 23.1 %all-to-all-start.9 = ((bf16[4,768,256]{2,1,0:T(8,128)(2,1)}), bf16[4,768,256]{2,1,0:T(8,128)(2,1)S(1)}, u32[]{:S(2)}, u32[]{:S(2)}) async-start(bf16[4,768,256]{2,1,0:T(8,128)(2,1)} %broadcast_in_dim.80), calls=%async_computation.9 | async-start | bytes 3145728 | tf_op jit(solution)/shard_map/all_to_all | solution.py:24
  517.2 10.5 %all-to-all-start.7 = ((bf16[4,2,2048]{2,1,0:T(2,128)(2,1)}), bf16[4,2,2048]{2,1,0:T(2,128)(2,1)S(1)}, u32[]{:S(2)}, u32[]{:S(2)}) async-start(bf16[4,2,2048]{2,1,0:T(2,128)(2,1)} %convert_element_type.64), calls=%async_computation.7 | async-start | bytes 65536 | tf_op jit(solution)/shard_map/all_to_all | solution.py:172
  (25 other events, 44.5 us)
Sparse Core Ops, SparseCore 0:
  29.9 95.0 all-gather.1
where the time goes:
time: 540 us; the launch traced here: 537 us
  waiting for transfers between devices  238 us (44%)
  matrix products  92 us (17%)
  blocking collectives  59.2 us (11%)
  local copies, waits for them, and re-layouts  48.3 us (9%)
  starting transfers between devices  48.2 us (9%)
  loops' own time  24.8 us (5%)
  between operations  14.4 us (3%)
  other arithmetic  11.2 us (2%)
    all_gather x1, waiting for transfers between devices, in_one_piece(): result, at, outs = (lax.all_gather(both, axis, axis=dim, tiled=True), 0, [])  93 us
    all_to_all x1, waiting for transfers between devices, per_device(): lax.all_to_all(sent[0], 'mem', split_axis=0, concat_axis=0, tiled=True)  50.4 us
    all_gather x1, blocking collectives, in_one_piece(): result, at, outs = (lax.all_gather(both, axis, axis=dim, tiled=True), 0, [])  46.2 us
    all_to_all x2, waiting for transfers between devices, sent_to_all(): lax.all_to_all(jnp.broadcast_to(array[None], (count, *array.shape)), axis...  38.3 us
    all_to_all x1, waiting for transfers between devices, sent_and_summed(): lax.all_to_all(pieces, axis, split_axis=0, concat_axis=0, tiled=True)  31.6 us
    dot_general x12, matrix products, frame_scores(): jnp.einsum('rghd,jgd->rghj', query_four, key_block, preferred_element_typ...  21.3 us
    dot_general x6, matrix products, forward_step(): jnp.einsum('rghj,jgd->rghd', weight.astype(jnp.bfloat16), value_block, pr...  20.9 us
    dot_general x6, matrix products, backward_step(): jnp.einsum('rghj,jgd->rghd', score_grad, key_block, preferred_element_typ...  19.1 us
  transfers between devices with their start and end apart: 10, of which 9 were waited for; matrix products, arithmetic and copies ran while one was open for 18% of the time, Pallas kernels for 0%

commit v1 on v0

--- a/solution.py
+++ b/solution.py
@@ -8,6 +8,15 @@
 HEAD_WIDTH = 128
 FRAME = 128
 masked_score = -1e30
+
+
+def follow_files(t0, ax_name):
+    now = jax.lax.axis_size(ax_name)
+    current_value = jnp.split(t0, now, axis=1)
+    spare = jnp.stack(current_value)
+    y = jax.lax.all_to_all(spare, ax_name, split_axis=0, concat_axis=0)
+    f_now = jnp.concatenate(y, axis=0)
+    return f_now
 
 
 def in_one_piece(arrays, axis, dim, along):
@@ -54,7 +63,7 @@
     mem_count = lax.axis_size("mem")
     local_query, local_grad = (
         lax.all_to_all(queries, "kvh", split_axis=1, concat_axis=0, tiled=True),
-        lax.all_to_all(output_gradient, "kvh", split_axis=1, concat_axis=0, tiled=True),
+        follow_files(output_gradient, "kvh"),
     )
     query_rows, grad_rows = in_one_piece((local_query, local_grad), "mem", 0, 1)
     group_size = query_rows.shape[0]

time: 540 us -> 540 us (level)
  blocking collectives: 59.2 us -> 46.2 us
  starting transfers between devices: 48.2 us -> 55.6 us
    all_to_all x1 -> x0, blocking collectives: 13.1 us -> none  [per_device(): lax.all_to_all(output_gradient, 'kvh', split_axis=1, concat_axis=0, tiled...]
    all_to_all x0 -> x1, waiting for transfers between devices: none -> 5.55 us  [follow_files(): y = jax.lax.all_to_all(spare, ax_name, split_axis=0, concat_axis=0)]
  transfers between devices with their start and end apart: 10 -> 11, of which waited for: 9 -> 10; matrix products, arithmetic and copies ran while one was open for 18% -> 18% of each run, Pallas kernels for 0% -> 0%
where the time goes in v1:
time: 540 us; the launch traced here: 537 us
  waiting for transfers between devices  243 us (45%)
  matrix products  92 us (17%)
  starting transfers between devices  55.6 us (10%)
  local copies, waits for them, and re-layouts  49.1 us (9%)
  blocking collectives  46.2 us (9%)
  loops' own time  24.8 us (5%)
  between operations  14.4 us (3%)
  other arithmetic  11.9 us (2%)
    all_gather x1, waiting for transfers between devices, in_one_piece(): result, at, outs = (lax.all_gather(both, axis, axis=dim, tiled=True), 0, [])  93 us
    all_to_all x1, waiting for transfers between devices, per_device(): lax.all_to_all(sent[0], 'mem', split_axis=0, concat_axis=0, tiled=True)  50.5 us
    all_gather x1, blocking collectives, in_one_piece(): result, at, outs = (lax.all_gather(both, axis, axis=dim, tiled=True), 0, [])  46.2 us
    all_to_all x2, waiting for transfers between devices, sent_to_all(): lax.all_to_all(jnp.broadcast_to(array[None], (count, *array.shape)), axis...  38.3 us
    all_to_all x1, waiting for transfers between devices, sent_and_summed(): lax.all_to_all(pieces, axis, split_axis=0, concat_axis=0, tiled=True)  31.6 us
    dot_general x12, matrix products, frame_scores(): jnp.einsum('rghd,jgd->rghj', query_four, key_block, preferred_element_typ...  21.3 us
    dot_general x6, matrix products, forward_step(): jnp.einsum('rghj,jgd->rghd', weight.astype(jnp.bfloat16), value_block, pr...  20.9 us
    dot_general x6, matrix products, backward_step(): jnp.einsum('rghj,jgd->rghd', score_grad, key_block, preferred_element_typ...  19.1 us
  transfers between devices with their start and end apart: 11, of which 10 were waited for; matrix products, arithmetic and copies ran while one was open for 18% of the time, Pallas kernels for 0%

profile of v1, /device:TPU:8, one launch (start us, length us, event | category | flops | bytes accessed | tf_op | source)
XLA Modules:
  0.0 536.6 jit_solution(8106337823995075407)
XLA Ops:
  7.2 7.4 %all-to-all-start = ((bf16[2,4,2048]{2,0,1:T(2,128)(2,1)}), bf16[2,4,2048]{2,0,1:T(2,128)(2,1)S(1)}, u32[]{:S(2)}, u32[]{:S(2)}) async-start(bf16[2,4,2048]{2,0,1:T(2,128)(2,1)} %bitcast.202), calls=%async_computation | async-start | bytes 65536 | tf_op jit(solution)/shard_map/all_to_all | solution.py:65
  16.0 4.2 all-to-all-done
  23.6 5.5 %all-to-all-done.1 = bf16[4,2,2048]{2,1,0:T(2,128)(2,1)S(1)} async-done(((bf16[4,2,2048]{2,1,0:T(2,128)(2,1)}), bf16[4,2,2048]{2,1,0:T(2,128)(2,1)S(1)}, u32[]{:S(2)}, u32[]{:S(2)}) %all-to-all-start.1) | async-done | bytes 32800 | tf_op jit(solution)/shard_map/all_to_all | solution.py:17
  32.0 93.0 %all-gather.2.cloned.1.call-done = bf16[256,4096]{1,0:T(8,128)(2,1)} async-done(((bf16[8,4096]{1,0:T(8,128)(2,1)}), bf16[256,4096]{1,0:T(8,128)(2,1)}) %all-gather.2.cloned.1.call-update) | async-done | bytes 2097168 | tf_op jit(solution)/shard_map/all_gather | solution.py:24
  129.6 50.9 %while.30 = (s32[]{:T(128)}, f32[256,2,8]{0,2,1:T(8,128)S(1)}, f32[256,2,8]{0,2,1:T(8,128)S(1)}, f32[256,2,8,128]{0,3,2,1:T(8,128)}, s32[6]{0:T(128)S(1)}, /*ind...) while((s32[]{:T(128)}, f32[256,2,8]{0,2,1:T(8,128)S(1)}, ...), condition=%wide.region_5.6_spmd.clone, body=%wide.region_2.5_spmd.clone.sunk | while | flops 276844544 | bytes 12191419 | solution.py:114
  141.8 3.7 bitcast_add_fusion.4
  150.6 3.7 bitcast_add_fusion.4
  168.1 3.7 bitcast_add_fusion.4
  176.8 3.7 bitcast_add_fusion.4
  183.3 5.6 %all-to-all-start.3 = ((f32[32,1,128]{2,1,0:T(1,128)}), f32[32,1,128]{2,1,0:T(1,128)S(1)}, u32[]{:S(2)}, u32[]{:S(2)}) async-start(f32[32,1,128]{2,1,0:T(1,128)} %reshape.133), calls=%async_computation.3 | async-start | bytes 32768 | tf_op jit(solution)/shard_map/all_to_all | solution.py:125
  191.7 8.3 %all-to-all-done.3 = f32[32,1,128]{2,1,0:T(1,128)S(1)} async-done(((f32[32,1,128]{2,1,0:T(1,128)}), f32[32,1,128]{2,1,0:T(1,128)S(1)}, u32[]{:S(2)}, u32[]{:S(2)}) %all-to-all-start.3) | async-done | bytes 16416 | tf_op jit(solution)/shard_map/all_to_all | solution.py:125
  200.0 4.9 all-to-all-start.4
  206.9 9.2 %all-to-all-done.4 = f32[32,1,128]{2,1,0:T(1,128)S(1)} async-done(((f32[32,1,128]{2,1,0:T(1,128)}), f32[32,1,128]{2,1,0:T(1,128)S(1)}, u32[]{:S(2)}, u32[]{:S(2)}) %all-to-all-start.4) | async-done | bytes 16416 | tf_op jit(solution)/shard_map/all_to_all | solution.py:126
  216.7 5.1 all-to-all-start.2
  228.6 50.5 %all-to-all-done.2 = f32[32,8,2,8,128]{4,3,2,1,0:T(8,128)S(1)} async-done(((f32[32,8,2,8,128]{4,3,2,1,0:T(8,128)}), f32[32,8,2,8,128]{4,3,2,1,0:T(8,128)S(1)}, u32[]{:S(2)}, u32[]{:S(2)}) %all-to-all-start.2) | async-done | bytes 2097184 | tf_op jit(solution)/shard_map/all_to_all | solution.py:124
  280.1 46.2 %all_gather.7 = f32[256,4,8]{2,1,0:T(4,128)S(1)} all-gather(f32[8,4,8]{2,1,0:T(4,128)S(1)} %copy.126), channel_id=1, replica_groups=mesh['mem'=32,'kvh'=4,'row'=4] {'mem'}, dimensions={0}, use_global_device_ids=true | all-gather | bytes 33792 | tf_op jit(solution)/shard_map/all_gather | solution.py:24
  327.3 3.9 all-to-all-start.5
  331.2 87.4 %while.31 = (s32[]{:T(128)}, f32[256,2,8,128]{0,3,2,1:T(8,128)}, bf16[6,128,2,128]{3,1,2,0:T(8,128)(2,1)}, bf16[6,128,2,128]{3,1,2,0:T(8,128)(2,1)}, s32[6]{0:T(...) while((s32[]{:T(128)}, f32[256,2,8,128]{0,3,2,1:T(8,128)}, ...), condition=%wide.region_11.12_spmd.clone, body=%wide.region_10.11_spmd.clone.sunk | while | flops 676888576 | bytes 22776864 | solution.py:166
  421.4 4.5 all-to-all-start.8
  427.8 19.5 %all-to-all-done.8 = bf16[4,768,256]{2,1,0:T(8,128)(2,1)} async-done(((bf16[4,768,256]{2,1,0:T(8,128)(2,1)}), bf16[4,768,256]{2,1,0:T(8,128)(2,1)}, u32[]{:S(2)}, u32[]{:S(2)}) %all-to-all-start.8) | async-done | bytes 1572896 | tf_op jit(solution)/shard_map/all_to_all | solution.py:33
  447.3 12.5 %all-to-all-start.6 = ((bf16[32,8,2,8,128]{4,3,2,1,0:T(8,128)(2,1)}), bf16[32,8,2,8,128]{4,3,2,1,0:T(8,128)(2,1)S(1)}, u32[]{:S(2)}, u32[]{:S(2)}) async-start(bf16[32,8,2,8,128]{4,3,2,1,0:T(8,128)(2,1)} %bitcast.12), calls=%async_computation.6 | async-start | bytes 2097152 | tf_op jit(solution)/shard_map/all_to_all | solution.py:50
  461.2 31.6 %all-to-all-done.6 = bf16[32,8,2,8,128]{4,3,2,1,0:T(8,128)(2,1)S(1)} async-done(((bf16[32,8,2,8,128]{4,3,2,1,0:T(8,128)(2,1)}), bf16[32,8,2,8,128]{4,3,2,1,0:T(8,128)(2,1)S(1)}, u32[]{:S(2)}, u32[]{:S(2)}) %all-to-all-start.6) | async-done | bytes 1048608 | tf_op jit(solution)/shard_map/all_to_all | solution.py:50
  498.5 18.8 %all-to-all-done.9 = bf16[4,768,256]{2,1,0:T(8,128)(2,1)S(1)} async-done(((bf16[4,768,256]{2,1,0:T(8,128)(2,1)}), bf16[4,768,256]{2,1,0:T(8,128)(2,1)S(1)}, u32[]{:S(2)}, u32[]{:S(2)}) %all-to-all-start.9) | async-done | bytes 1572896 | tf_op jit(solution)/shard_map/all_to_all | solution.py:33
  517.2 4.8 all-to-all-start.7
  (257 shorter events, 146.9 us)
Async XLA Ops:
  7.2 23.9 %copy-start.4 = (bf16[768,256]{1,0:T(8,128)(2,1)S(1)}, bf16[768,256]{1,0:T(8,128)(2,1)}, u32[]{:S(2)}) copy-start(bf16[768,256]{1,0:T(8,128)(2,1)} %param.13) | copy-start | bytes 1179652
  7.2 24.0 %copy-start.11 = (s32[96]{0:T(128)S(1)}, s32[96]{0:T(128)}, u32[]{:S(2)}) copy-start(s32[96]{0:T(128)} %param.15) | copy-start | bytes 1156
  7.2 24.3 %copy-start.10 = (s32[128,2]{0,1:T(2,128)S(1)}, s32[128,2]{0,1:T(2,128)}, u32[]{:S(2)}) copy-start(s32[128,2]{0,1:T(2,128)} %param.14) | copy-start | bytes 3076
  7.2 13.1 %all-to-all-start = ((bf16[2,4,2048]{2,0,1:T(2,128)(2,1)}), bf16[2,4,2048]{2,0,1:T(2,128)(2,1)S(1)}, u32[]{:S(2)}, u32[]{:S(2)}) async-start(bf16[2,4,2048]{2,0,1:T(2,128)(2,1)} %bitcast.202), calls=%async_computation | async-start | bytes 65536 | tf_op jit(solution)/shard_map/all_to_all | solution.py:65
  20.3 8.9 %all-to-all-start.1 = ((bf16[4,2,2048]{2,1,0:T(2,128)(2,1)}), bf16[4,2,2048]{2,1,0:T(2,128)(2,1)S(1)}, u32[]{:S(2)}, u32[]{:S(2)}) async-start(bf16[4,2,2048]{2,1,0:T(2,128)(2,1)} %pad_maximum_fusion.1), calls=%async_computation.1 | async-start | bytes 65536 | tf_op jit(solution)/shard_map/all_to_all | solution.py:17
  23.5 101.5 %all-gather.2.cloned.1.call-start = ((), (), s32[]{:S(2)}) async-start(), calls=%async_computation.10 | async-start | bytes 2162688 | tf_op jit(solution)/shard_map/all_gather | solution.py:24
  180.6 26.4 %copy-start.3 = (bf16[6,128,2,128]{3,2,1,0:T(2,128)(2,1)}, bf16[6,128,2,128]{3,2,1,0:T(2,128)(2,1)S(1)}, u32[]{:S(2)}) copy-start(bf16[6,128,2,128]{3,2,1,0:T(2,128)(2,1)S(1)} %get-tuple-element.598) | copy-start | bytes 1179652
  180.6 26.4 %copy-start.6 = (pred[256,6]{0,1:T(8,128)(4,1)}, pred[256,6]{0,1:T(8,128)(4,1)S(1)}, u32[]{:S(2)}) copy-start(pred[256,6]{0,1:T(8,128)(4,1)S(1)} %get-tuple-element.605) | copy-start | bytes 4612
  180.6 24.4 %copy-start.2 = (f32[256,2,8,128]{0,3,2,1:T(8,128)S(1)}, f32[256,2,8,128]{0,3,2,1:T(8,128)}, u32[]{:S(2)}) copy-start(f32[256,2,8,128]{0,3,2,1:T(8,128)} %get-tuple-element.117) | copy-start | bytes 6291460
  183.3 16.7 %all-to-all-start.3 = ((f32[32,1,128]{2,1,0:T(1,128)}), f32[32,1,128]{2,1,0:T(1,128)S(1)}, u32[]{:S(2)}, u32[]{:S(2)}) async-start(f32[32,1,128]{2,1,0:T(1,128)} %reshape.133), calls=%async_computation.3 | async-start | bytes 32768 | tf_op jit(solution)/shard_map/all_to_all | solution.py:125
  200.0 16.1 %all-to-all-start.4 = ((f32[32,1,128]{2,1,0:T(1,128)}), f32[32,1,128]{2,1,0:T(1,128)S(1)}, u32[]{:S(2)}, u32[]{:S(2)}) async-start(f32[32,1,128]{2,1,0:T(1,128)} %reshape.135), calls=%async_computation.4 | async-start | bytes 32768 | tf_op jit(solution)/shard_map/all_to_all | solution.py:126
  216.7 62.3 %all-to-all-start.2 = ((f32[32,8,2,8,128]{4,3,2,1,0:T(8,128)}), f32[32,8,2,8,128]{4,3,2,1,0:T(8,128)S(1)}, u32[]{:S(2)}, u32[]{:S(2)}) async-start(f32[32,8,2,8,128]{4,3,2,1,0:T(8,128)} %bitcast.191), calls=%async_computation.2 | async-start | bytes 4194304 | tf_op jit(solution)/shard_map/all_to_all | solution.py:124
  228.2 51.5 %copy-start.5 = (f32[8,2,8,128]{3,2,1,0:T(8,128)S(1)}, f32[8,2,8,128]{3,2,1,0:T(8,128)}, u32[]{:S(2)}) copy-start(f32[8,2,8,128]{3,2,1,0:T(8,128)} %reshape.122) | copy-start | bytes 196612
  327.3 92.8 %all-to-all-start.5 = ((bf16[4,2,2048]{2,1,0:T(2,128)(2,1)}), bf16[4,2,2048]{2,1,0:T(2,128)(2,1)}, u32[]{:S(2)}, u32[]{:S(2)}) async-start(bf16[4,2,2048]{2,1,0:T(2,128)(2,1)} %convert_element_type.60), calls=%async_computation.5 | async-start | bytes 65536 | tf_op jit(solution)/shard_map/all_to_all | solution.py:180
  331.2 6.2 %copy-start.8 = (f32[256,2,8]{0,2,1:T(8,128)}, f32[256,2,8]{0,2,1:T(8,128)S(1)}, u32[]{:S(2)}) copy-start(f32[256,2,8]{0,2,1:T(8,128)S(1)} %get-tuple-element.574) | copy-start | bytes 49156 | tf_op jit(solution)/shard_map/while
  344.5 6.2 %copy-start.8 = (f32[256,2,8]{0,2,1:T(8,128)}, f32[256,2,8]{0,2,1:T(8,128)S(1)}, u32[]{:S(2)}) copy-start(f32[256,2,8]{0,2,1:T(8,128)S(1)} %get-tuple-element.574) | copy-start | bytes 49156 | tf_op jit(solution)/shard_map/while
  359.3 6.2 %copy-start.8 = (f32[256,2,8]{0,2,1:T(8,128)}, f32[256,2,8]{0,2,1:T(8,128)S(1)}, u32[]{:S(2)}) copy-start(f32[256,2,8]{0,2,1:T(8,128)S(1)} %get-tuple-element.574) | copy-start | bytes 49156 | tf_op jit(solution)/shard_map/while
  374.1 6.2 %copy-start.8 = (f32[256,2,8]{0,2,1:T(8,128)}, f32[256,2,8]{0,2,1:T(8,128)S(1)}, u32[]{:S(2)}) copy-start(f32[256,2,8]{0,2,1:T(8,128)S(1)} %get-tuple-element.574) | copy-start | bytes 49156 | tf_op jit(solution)/shard_map/while
  388.9 6.2 %copy-start.8 = (f32[256,2,8]{0,2,1:T(8,128)}, f32[256,2,8]{0,2,1:T(8,128)S(1)}, u32[]{:S(2)}) copy-start(f32[256,2,8]{0,2,1:T(8,128)S(1)} %get-tuple-element.574) | copy-start | bytes 49156 | tf_op jit(solution)/shard_map/while
  403.8 6.2 %copy-start.8 = (f32[256,2,8]{0,2,1:T(8,128)}, f32[256,2,8]{0,2,1:T(8,128)S(1)}, u32[]{:S(2)}) copy-start(f32[256,2,8]{0,2,1:T(8,128)S(1)} %get-tuple-element.574) | copy-start | bytes 49156 | tf_op jit(solution)/shard_map/while
  421.4 25.9 %all-to-all-start.8 = ((bf16[4,768,256]{2,1,0:T(8,128)(2,1)}), bf16[4,768,256]{2,1,0:T(8,128)(2,1)}, u32[]{:S(2)}, u32[]{:S(2)}) async-start(bf16[4,768,256]{2,1,0:T(8,128)(2,1)} %broadcast_in_dim.79), calls=%async_computation.8 | async-start | bytes 3145728 | tf_op jit(solution)/shard_map/all_to_all | solution.py:33
  447.3 45.6 %all-to-all-start.6 = ((bf16[32,8,2,8,128]{4,3,2,1,0:T(8,128)(2,1)}), bf16[32,8,2,8,128]{4,3,2,1,0:T(8,128)(2,1)S(1)}, u32[]{:S(2)}, u32[]{:S(2)}) async-start(bf16[32,8,2,8,128]{4,3,2,1,0:T(8,128)(2,1)} %bitcast.12), calls=%async_computation.6 | async-start | bytes 2097152 | tf_op jit(solution)/shard_map/all_to_all | solution.py:50
  494.1 23.1 %all-to-all-start.9 = ((bf16[4,768,256]{2,1,0:T(8,128)(2,1)}), bf16[4,768,256]{2,1,0:T(8,128)(2,1)S(1)}, u32[]{:S(2)}, u32[]{:S(2)}) async-start(bf16[4,768,256]{2,1,0:T(8,128)(2,1)} %broadcast_in_dim.80), calls=%async_computation.9 | async-start | bytes 3145728 | tf_op jit(solution)/shard_map/all_to_all | solution.py:33
  517.2 10.5 %all-to-all-start.7 = ((bf16[4,2,2048]{2,1,0:T(2,128)(2,1)}), bf16[4,2,2048]{2,1,0:T(2,128)(2,1)S(1)}, u32[]{:S(2)}, u32[]{:S(2)}) async-start(bf16[4,2,2048]{2,1,0:T(2,128)(2,1)} %convert_element_type.64), calls=%async_computation.7 | async-start | bytes 65536 | tf_op jit(solution)/shard_map/all_to_all | solution.py:181
  (26 other events, 50.4 us)
Sparse Core Ops, SparseCore 0:
  29.9 95.0 all-gather.1
